TPU v7x, 32 devices: a whole 2x2x4 slice. The times are simulated.
32 devices in a mesh: dp: 4 (over y, x), tp: 8 (over z, core).
Axes of the slice: x: 2, y: 2, z: 4, core: 2. Of those that a mesh axis runs over, the one named last changes fastest.
Arguments:
- gradients: bfloat16 [4, 4, 3072, 768], P('dp', None, 'tp'), may hold values from -6 to 6, as said below
- right_factor: float32 [4, 768, 8], replicated, may hold values from -6 to 6
- weights_before: float32 [4, 3072, 768], P(None, 'tp', 'dp'), may hold values from -0.21875 to 0.21875
- momentum: float32 [4, 3072, 768], P(None, 'tp', 'dp'), may hold values from -0.3125 to 0.3125
Outputs:
- new_weights: float32 [4, 3072, 768], P(None, 'tp', 'dp')
- new_basis: float32 [4, 768, 8], replicated
- new_momentum: float32 [4, 3072, 768], P(None, 'tp', 'dp')
Inputs may be any that keep to these rules, and one draw needn't show every extreme that they name: gradients holds numbers from -6 to 6.
All inputs are finite; a program needn't handle non-finite values.
Results may differ from a plain program's by a relative error of at most 0.0003.
Values sent between devices are 32-bit elements.
A program may use at most 64 MiB of HBM per device.

v0:
```python
import jax
import jax.numpy as jnp
from jax import lax
from jax.sharding import PartitionSpec as P

RANK = 8


def on_device(gradients, right_factor, weights_before, momentum):
    own_grads = gradients[0]
    part_left = jnp.einsum(
        "liw,lwr->lir",
        own_grads,
        right_factor.astype(jnp.bfloat16),
        preferred_element_type=jnp.float32,
    )
    left = lax.psum(part_left, "dp")
    part_gram = jnp.einsum("lir,lis->lrs", left, left, precision=lax.Precision.HIGHEST)
    small_left = left.astype(jnp.bfloat16)
    part_right = jnp.einsum(
        "liw,lir->lwr", own_grads, small_left, preferred_element_type=jnp.float32
    )
    own_share = part_gram / lax.axis_size("dp")
    right, gram = lax.psum((part_right, own_share), ("dp", "tp"))
    gram = gram + 0.001 * jnp.mean(jnp.diagonal(gram, axis1=1, axis2=2), axis=1)[
        :, None, None
    ] * jnp.eye(RANK, dtype=jnp.float32)
    place = lax.axis_index("dp") * weights_before.shape[2]
    own_right = lax.dynamic_slice_in_dim(right, place, weights_before.shape[2], axis=1)
    root = jnp.linalg.cholesky(gram)
    half = lax.linalg.triangular_solve(
        root, jnp.swapaxes(own_right, 1, 2), left_side=True, lower=True
    )
    mixed = lax.linalg.triangular_solve(root, half, left_side=True, lower=True, transpose_a=True)
    change = jnp.einsum(
        "lir,lrw->liw", left, mixed, precision=lax.Precision.HIGHEST
    ) / lax.axis_size("dp")
    new_momentum = 0.9 * momentum + change
    new_weights = weights_before - 0.02 * new_momentum
    new_basis = right * lax.rsqrt(jnp.mean(right * right, axis=(1, 2), keepdims=True) + 1e-12)
    return (new_weights, new_basis, new_momentum)


def solution(mesh):
    in_specs = (P("dp", None, "tp", None), P(), P(None, "tp", "dp"), P(None, "tp", "dp"))
    out_specs = (P(None, "tp", "dp"), P(), P(None, "tp", "dp"))
    return jax.shard_map(
        on_device, mesh=mesh, in_specs=in_specs, out_specs=out_specs, check_vma=False
    )
```

profile of v0, /device:TPU:8, one launch (start us, length us, event | category | flops | bytes accessed | tf_op | source)
XLA Modules:
  0.0 166.5 jit_solution(5481928536512770521)
XLA Ops:
  7.2 0.0 copy-start
  7.2 0.0 all-reduce.2.cloned.1.call-start
  7.2 1.6 copy-done
  8.8 1.6 fusion.2
  10.4 16.7 %psum.21 = f32[4,384,8]{1,2,0:T(8,128)S(1)} all-reduce(f32[4,384,8]{1,2,0:T(8,128)S(1)} %fusion.2), channel_id=1, replica_groups=mesh['dp'=4,'tp'=8] {'dp'}, use_global_device_ids=true, to_apply=%region_0.0 | all-reduce | flops 12288 | bytes 98304 | tf_op jit(solution)/shard_map/psum | solution.py:17
  27.1 1.1 fusion.5
  28.2 0.0 all-reduce.2.cloned.1.call-update
  28.3 0.2 convolution_multiply_fusion.1
  28.5 0.1 copy.13
  28.5 39.5 %psum.22 = f32[4,8,8]{1,2,0:T(8,128)S(1)} all-reduce(f32[4,8,8]{1,2,0:T(8,128)S(1)} %convolution_multiply_fusion.1), channel_id=1, replica_groups=mesh['dp'=4,'tp'=8] {'dp','tp'}, use_global_device_ids=true, to_apply=%region_1.0 | all-reduce | flops 256 | bytes 2048 | tf_op jit(solution)/shard_map/psum | solution.py:24
  68.0 0.1 copy.12
  68.1 0.6 gather_fusion
  68.7 0.1 multiply_add_fusion
  68.8 0.1 copy.14
  68.9 0.1 fusion.15
  69.0 2.9 %custom-call.9 = f32[4,8,8]{2,1,0:T(8,128)S(1)} custom-call(f32[4,8,8]{2,1,0:T(8,128)S(1)} %fusion.15), custom_call_target="Cholesky" | custom-call | tf_op jit(solution)/shard_map/jit(cholesky)/cholesky | solution.py:30
  71.9 0.1 select_reduce_fusion
  71.9 0.1 compare_reduce_fusion
  72.0 0.1 select_bitcast_fusion
  72.1 2.5 %custom-call.10 = f32[4,1,8,8]{2,3,1,0:T(8,128)S(1)} custom-call(f32[4,1,8,8]{3,2,1,0:T(8,128)S(1)} %select_bitcast_fusion), custom_call_target="InvertDiagBlocksLowerTriangular" | custom-call | tf_op jit(solution)/shard_map/triangular_solve | solution.py:34
  74.6 77.7 %all-reduce.2.cloned.1.call-done = f32[4,768,8]{1,2,0:T(8,128)} async-done(((f32[4,768,8]{1,2,0:T(8,128)}), f32[4,768,8]{1,2,0:T(8,128)}) %all-reduce.2.cloned.1.call-update) | async-done | bytes 98320 | tf_op jit(solution)/shard_map/psum | solution.py:24
  152.3 1.0 multiply_reduce_fusion
  153.3 1.1 fusion.9
  154.4 0.2 fusion.12
  154.5 0.0 copy-start.1
  154.5 4.4 %multiply_subtract_fusion = (f32[4,384,192]{1,2,0:T(8,128)}, f32[4,384,192]{1,2,0:T(8,128)}) fusion(f32[4,384,192]{1,2,0:T(8,128)} %param.6, f32[4,384,8]{1,2,0:T(8,128)S(1)} %psum.21, f32[4,8,192]{2,1,0:T(8,128)S(1)} %fusion.12, f32[4,384,192]{1,2,0:T(8,128)} %param.7), kind=kOutput, calls=%fused_computation.7 | convolution fusion | flops 29786112 | bytes 4792320 | tf_op jit(solution)/shard_map/lir,lrw->liw/dot_general | solution.py:35
  158.9 0.0 copy-done.1
  158.9 0.7 broadcast_multiply_fusion
  (7 shorter events, 0.1 us)
Async XLA Ops:
  7.2 1.7 %copy-start = (bf16[1,4,384,768]{3,2,1,0:T(8,128)(2,1)S(1)}, bf16[1,4,384,768]{3,2,1,0:T(8,128)(2,1)}, u32[]{:S(2)}) copy-start(bf16[1,4,384,768]{3,2,1,0:T(8,128)(2,1)} %param.4) | copy-start | bytes 7077892
  7.2 145.1 %all-reduce.2.cloned.1.call-start = ((), (), s32[]{:S(2)}) async-start(), calls=%async_computation | async-start | bytes 196608 | tf_op jit(solution)/shard_map/psum | solution.py:24
  154.5 4.4 %copy-start.1 = (f32[4,768,8]{1,2,0:T(8,128)S(1)}, f32[4,768,8]{1,2,0:T(8,128)}, u32[]{:S(2)}) copy-start(f32[4,768,8]{1,2,0:T(8,128)} %all-reduce.2.cloned.1.call-done) | copy-start | bytes 294916
Sparse Core Ops, SparseCore 0:
  28.3 123.8 all-reduce.1
where the time goes:
time: 167 us; the launch traced here: 166 us
  waiting for transfers between devices  77.7 us (47%)
  blocking collectives  56.2 us (34%)
  between operations  14.1 us (8%)
  matrix products  8.45 us (5%)
  other arithmetic  7.59 us (5%)
  local copies, waits for them, and re-layouts  2.47 us (1%)
    psum x1, waiting for transfers between devices, on_device(): right, gram = lax.psum((part_right, own_share), ('dp', 'tp'))  77.7 us
    psum x1, blocking collectives, on_device(): right, gram = lax.psum((part_right, own_share), ('dp', 'tp'))  39.5 us
    psum x1, blocking collectives, on_device(): left = lax.psum(part_left, 'dp')  16.7 us
    dot_general x1, matrix products, on_device(): jnp.einsum('lir,lrw->liw', left, mixed, precision=lax.Precision.HIGHEST)  4.38 us
  transfers between devices with their start and end apart: 1, of which 1 were waited for; matrix products, arithmetic and copies ran while one was open for 4% of the time, Pallas kernels for 0%

commit v1 on v0

--- a/solution.py
+++ b/solution.py
@@ -4,6 +4,11 @@
 from jax.sharding import PartitionSpec as P
 
 RANK = 8
+
+
+def one_after_other(value, axis_one, axis_two):
+    partial = lax.psum(value, axis_one)
+    return lax.psum(partial, axis_two)
 
 
 def on_device(gradients, right_factor, weights_before, momentum):
@@ -21,7 +26,7 @@
         "liw,lir->lwr", own_grads, small_left, preferred_element_type=jnp.float32
     )
     own_share = part_gram / lax.axis_size("dp")
-    right, gram = lax.psum((part_right, own_share), ("dp", "tp"))
+    right, gram = one_after_other((part_right, own_share), "dp", "tp")
     gram = gram + 0.001 * jnp.mean(jnp.diagonal(gram, axis1=1, axis2=2), axis=1)[
         :, None, None
     ] * jnp.eye(RANK, dtype=jnp.float32)

time: 167 us -> 141 us (0.84)
  waiting for transfers between devices: 77.7 us -> 54.7 us
  blocking collectives: 56.2 us -> 53 us
    psum x1 -> x2, waiting for transfers between devices: 77.7 us -> 54.7 us  [the longest x1 53.8 us: one_after_other(): return lax.psum(partial, axis_two)]
    psum x1 -> x2, blocking collectives: 39.5 us -> 36.3 us  [the longest x1 22.4 us: one_after_other(): return lax.psum(partial, axis_two)]
  transfers between devices with their start and end apart: 1 -> 2, of which waited for: 1 -> 2; matrix products, arithmetic and copies ran while one was open for 4% -> 5% of each run, Pallas kernels for 0% -> 0%
where the time goes in v1:
time: 141 us; the launch traced here: 140 us
  waiting for transfers between devices  54.7 us (39%)
  blocking collectives  53 us (38%)
  between operations  14.1 us (10%)
  matrix products  8.45 us (6%)
  other arithmetic  7.6 us (5%)
  local copies, waits for them, and re-layouts  2.46 us (2%)
    psum x1, waiting for transfers between devices, one_after_other(): return lax.psum(partial, axis_two)  53.8 us
    psum x1, blocking collectives, one_after_other(): return lax.psum(partial, axis_two)  22.4 us
    psum x1, blocking collectives, on_device(): left = lax.psum(part_left, 'dp')  16.7 us
    psum x1, blocking collectives, one_after_other(): partial = lax.psum(value, axis_one)  13.9 us
    dot_general x1, matrix products, on_device(): jnp.einsum('lir,lrw->liw', left, mixed, precision=lax.Precision.HIGHEST)  4.38 us
    another operation x4, other arithmetic, on_device(): root = jnp.linalg.cholesky(gram)  3.09 us
  transfers between devices with their start and end apart: 2, of which 2 were waited for; matrix products, arithmetic and copies ran while one was open for 5% of the time, Pallas kernels for 0%

profile of v1, /device:TPU:8, one launch (start us, length us, event | category | flops | bytes accessed | tf_op | source)
XLA Modules:
  0.0 140.3 jit_solution(3946585352125908093)
XLA Ops:
  7.2 0.0 copy-start
  7.2 0.0 all-reduce.3.cloned.1.call-start
  7.2 1.6 %copy-done = bf16[1,4,384,768]{3,2,1,0:T(8,128)(2,1)S(1)} copy-done((bf16[1,4,384,768]{3,2,1,0:T(8,128)(2,1)S(1)}, bf16[1,4,384,768]{3,2,1,0:T(8,128)(2,1)}, u32[]{:S(2)}) %copy-start) | copy-done | bytes 2359320
  8.8 1.6 %fusion.2 = f32[4,384,8]{1,2,0:T(8,128)S(1)} fusion(bf16[1,4,384,768]{3,2,1,0:T(8,128)(2,1)S(1)} %copy-done, f32[4,768,8]{1,2,0:T(8,128)} %param.5), kind=kOutput, calls=%fused_computation.3 | convolution fusion | flops 18898944 | bytes 2506752 | tf_op jit(solution)/shard_map/liw,lwr->lir/dot_general | solution.py:16
  10.4 16.7 %psum.35 = f32[4,384,8]{1,2,0:T(8,128)S(1)} all-reduce(f32[4,384,8]{1,2,0:T(8,128)S(1)} %fusion.2), channel_id=1, replica_groups=mesh['dp'=4,'tp'=8] {'dp'}, use_global_device_ids=true, to_apply=%region_0.0 | all-reduce | flops 12288 | bytes 98304 | tf_op jit(solution)/shard_map/psum | solution.py:22
  27.1 1.1 fusion.5
  28.2 0.0 all-reduce.3.cloned.1.call-update
  28.2 0.0 all-reduce.5.cloned.1.call-start
  28.3 0.2 convolution_multiply_fusion.1
  28.5 0.1 copy.13
  28.6 13.9 %psum.36 = f32[4,8,8]{1,2,0:T(8,128)S(1)} all-reduce(f32[4,8,8]{1,2,0:T(8,128)S(1)} %convolution_multiply_fusion.1), channel_id=1, replica_groups=mesh['dp'=4,'tp'=8] {'dp'}, use_global_device_ids=true, to_apply=%region_1.0 | all-reduce | flops 256 | bytes 2048 | tf_op jit(solution)/shard_map/psum | solution.py:10
  42.5 22.4 %psum.37 = f32[4,8,8]{1,2,0:T(8,128)S(1)} all-reduce(f32[4,8,8]{1,2,0:T(8,128)S(1)} %psum.36), channel_id=1, replica_groups=mesh['dp'=4,'tp'=8] {'tp'}, use_global_device_ids=true, to_apply=%region_2.0 | all-reduce | flops 256 | bytes 2048 | tf_op jit(solution)/shard_map/psum | solution.py:11
  64.8 0.1 copy.12
  65.0 0.6 gather_fusion
  65.6 0.1 multiply_add_fusion
  65.6 0.1 copy.14
  65.7 0.1 fusion.15
  65.8 2.9 %custom-call.9 = f32[4,8,8]{2,1,0:T(8,128)S(1)} custom-call(f32[4,8,8]{2,1,0:T(8,128)S(1)} %fusion.15), custom_call_target="Cholesky" | custom-call | tf_op jit(solution)/shard_map/jit(cholesky)/cholesky | solution.py:35
  68.7 0.1 select_reduce_fusion
  68.8 0.1 compare_reduce_fusion
  68.9 0.9 all-reduce.3.cloned.1.call-done
  69.8 0.0 all-reduce.5.cloned.1.call-update
  69.8 0.1 select_bitcast_fusion
  69.9 2.5 %custom-call.10 = f32[4,1,8,8]{2,3,1,0:T(8,128)S(1)} custom-call(f32[4,1,8,8]{3,2,1,0:T(8,128)S(1)} %select_bitcast_fusion), custom_call_target="InvertDiagBlocksLowerTriangular" | custom-call | tf_op jit(solution)/shard_map/triangular_solve | solution.py:39
  72.4 53.8 %all-reduce.5.cloned.1.call-done = f32[4,768,8]{1,2,0:T(8,128)} async-done(((f32[4,768,8]{1,2,0:T(8,128)}), f32[4,768,8]{1,2,0:T(8,128)}) %all-reduce.5.cloned.1.call-update) | async-done | bytes 98320 | tf_op jit(solution)/shard_map/psum | solution.py:11
  126.1 1.0 multiply_reduce_fusion
  127.2 1.1 fusion.9
  128.2 0.2 fusion.12
  128.4 0.0 copy-start.1
  128.4 4.4 %multiply_subtract_fusion = (f32[4,384,192]{1,2,0:T(8,128)}, f32[4,384,192]{1,2,0:T(8,128)}) fusion(f32[4,384,192]{1,2,0:T(8,128)} %param.6, f32[4,384,8]{1,2,0:T(8,128)S(1)} %psum.35, f32[4,8,192]{2,1,0:T(8,128)S(1)} %fusion.12, f32[4,384,192]{1,2,0:T(8,128)} %param.7), kind=kOutput, calls=%fused_computation.7 | convolution fusion | flops 29786112 | bytes 4792320 | tf_op jit(solution)/shard_map/lir,lrw->liw/dot_general | solution.py:40
  132.8 0.0 copy-done.1
  132.8 0.7 broadcast_multiply_fusion
  (7 shorter events, 0.1 us)
Async XLA Ops:
  7.2 1.7 %copy-start = (bf16[1,4,384,768]{3,2,1,0:T(8,128)(2,1)S(1)}, bf16[1,4,384,768]{3,2,1,0:T(8,128)(2,1)}, u32[]{:S(2)}) copy-start(bf16[1,4,384,768]{3,2,1,0:T(8,128)(2,1)} %param.4) | copy-start | bytes 7077892
  7.2 62.6 %all-reduce.3.cloned.1.call-start = ((), (), s32[]{:S(2)}) async-start(), calls=%async_computation | async-start | bytes 196608 | tf_op jit(solution)/shard_map/psum | solution.py:10
  28.2 97.9 %all-reduce.5.cloned.1.call-start = ((), (), s32[]{:S(2)}) async-start(), calls=%async_computation.1 | async-start | bytes 196608 | tf_op jit(solution)/shard_map/psum | solution.py:11
  128.4 4.4 %copy-start.1 = (f32[4,768,8]{1,2,0:T(8,128)S(1)}, f32[4,768,8]{1,2,0:T(8,128)}, u32[]{:S(2)}) copy-start(f32[4,768,8]{1,2,0:T(8,128)} %all-reduce.5.cloned.1.call-done) | copy-start | bytes 294916
Sparse Core Ops, SparseCore 0:
  28.3 41.3 all-reduce.2
  72.1 54.0 all-reduce.4

commit v2 on v0

--- a/solution.py
+++ b/solution.py
@@ -4,6 +4,25 @@
 from jax.sharding import PartitionSpec as P
 
 RANK = 8
+
+
+def region_produce(local_x):
+    parts_n = lax.axis_size("dp")
+
+    def edit_unit(z1, side_arr):
+        if side_arr >= parts_n:
+            return z1
+        w1 = edit_unit(
+            z1
+            + lax.ppermute(
+                z1, "dp", list(map(lambda src_i: (src_i, src_i ^ side_arr), range(parts_n)))
+            ),
+            2 * side_arr,
+        )
+        return w1
+
+    main = edit_unit(local_x, 1)
+    return main
 
 
 def on_device(gradients, right_factor, weights_before, momentum):
@@ -14,7 +33,7 @@
         right_factor.astype(jnp.bfloat16),
         preferred_element_type=jnp.float32,
     )
-    left = lax.psum(part_left, "dp")
+    left = region_produce(part_left)
     part_gram = jnp.einsum("lir,lis->lrs", left, left, precision=lax.Precision.HIGHEST)
     small_left = left.astype(jnp.bfloat16)
     part_right = jnp.einsum(

time: 167 us -> 204 us (1.22)
  waiting for transfers between devices: 77.7 us -> 127 us
  blocking collectives: 56.2 us -> 40.5 us
  starting transfers between devices: 0.04 us -> 3.11 us
    psum x1, waiting for transfers between devices: 77.7 us -> 122 us  [on_device(): right, gram = lax.psum((part_right, own_share), ('dp', 'tp'))]
    psum x1 -> x0, blocking collectives: 16.7 us -> none  [on_device(): left = lax.psum(part_left, 'dp')]
    ppermute x0 -> x2, waiting for transfers between devices: none -> 5.07 us  [edit_unit(): lax.ppermute(z1, 'dp', list(map(lambda src_i: (src_i, src_i ^ side_arr),...]
    ppermute x0 -> x2, starting transfers between devices: none -> 3.08 us  [edit_unit(): lax.ppermute(z1, 'dp', list(map(lambda src_i: (src_i, src_i ^ side_arr),...]
  transfers between devices with their start and end apart: 1 -> 3, of which waited for: 1 -> 3; matrix products, arithmetic and copies ran while one was open for 4% -> 1% of each run, Pallas kernels for 0% -> 0%
where the time goes in v2:
time: 204 us; the launch traced here: 203 us
  waiting for transfers between devices  127 us (62%)
  blocking collectives  40.5 us (20%)
  between operations  14.1 us (7%)
  matrix products  8.46 us (4%)
  other arithmetic  7.6 us (4%)
  starting transfers between devices  3.11 us (2%)
  local copies, waits for them, and re-layouts  2.46 us (1%)
    psum x1, waiting for transfers between devices, on_device(): right, gram = lax.psum((part_right, own_share), ('dp', 'tp'))  122 us
    psum x1, blocking collectives, on_device(): right, gram = lax.psum((part_right, own_share), ('dp', 'tp'))  40.5 us
    ppermute x2, waiting for transfers between devices, edit_unit(): lax.ppermute(z1, 'dp', list(map(lambda src_i: (src_i, src_i ^ side_arr),...  5.07 us
    dot_general x1, matrix products, on_device(): jnp.einsum('lir,lrw->liw', left, mixed, precision=lax.Precision.HIGHEST)  4.38 us
  transfers between devices with their start and end apart: 3, of which 3 were waited for; matrix products, arithmetic and copies ran while one was open for 1% of the time, Pallas kernels for 0%

profile of v2, /device:TPU:8, one launch (start us, length us, event | category | flops | bytes accessed | tf_op | source)
XLA Modules:
  0.0 203.2 jit_solution(3978452308150643244)
XLA Ops:
  7.2 0.0 copy-start
  7.2 0.0 all-reduce.2.cloned.1.call-start
  7.2 1.6 copy-done
  8.8 1.6 fusion.2
  10.4 1.5 collective-permute-start
  11.9 2.6 %collective-permute-done = f32[4,384,8]{1,2,0:T(8,128)S(1)} collective-permute-done((f32[4,384,8]{1,2,0:T(8,128)S(1)}, f32[4,384,8]{1,2,0:T(8,128)S(1)}, u32[]{:S(2)}, u32[]{:S(2)}) %collective-permute-start) | collective-permute-done | bytes 49184 | tf_op jit(solution)/shard_map/ppermute | solution.py:17
  14.5 1.6 collective-permute-start.1
  16.1 0.1 copy.13
  16.2 2.5 %collective-permute-done.1 = f32[4,384,8]{1,2,0:T(8,128)S(1)} collective-permute-done((f32[4,384,8]{1,2,0:T(8,128)S(1)}, f32[4,384,8]{1,2,0:T(8,128)S(1)}, u32[]{:S(2)}, u32[]{:S(2)}) %collective-permute-start.1) | collective-permute-done | bytes 49184 | tf_op jit(solution)/shard_map/ppermute | solution.py:17
  18.7 0.2 convolution_multiply_fusion.1
  18.9 1.1 fusion.5
  20.0 40.5 %psum.14 = f32[4,8,8]{1,2,0:T(8,128)S(1)} all-reduce(f32[4,8,8]{1,2,0:T(8,128)S(1)} %convolution_multiply_fusion.1), channel_id=1, replica_groups=mesh['dp'=4,'tp'=8] {'dp','tp'}, use_global_device_ids=true, to_apply=%region_0.0 | all-reduce | flops 256 | bytes 2048 | tf_op jit(solution)/shard_map/psum | solution.py:43
  60.4 0.1 copy.12
  60.6 0.6 gather_fusion
  61.2 0.1 multiply_add_fusion
  61.2 0.1 copy.14
  61.3 0.1 fusion.15
  61.4 2.9 %custom-call.9 = f32[4,8,8]{2,1,0:T(8,128)S(1)} custom-call(f32[4,8,8]{2,1,0:T(8,128)S(1)} %fusion.15), custom_call_target="Cholesky" | custom-call | tf_op jit(solution)/shard_map/jit(cholesky)/cholesky | solution.py:49
  64.3 0.1 select_reduce_fusion
  64.3 0.1 compare_reduce_fusion
  64.5 0.0 all-reduce.2.cloned.1.call-update
  64.5 0.1 select_bitcast_fusion
  64.6 2.5 %custom-call.10 = f32[4,1,8,8]{2,3,1,0:T(8,128)S(1)} custom-call(f32[4,1,8,8]{3,2,1,0:T(8,128)S(1)} %select_bitcast_fusion), custom_call_target="InvertDiagBlocksLowerTriangular" | custom-call | tf_op jit(solution)/shard_map/triangular_solve | solution.py:53
  67.1 121.9 %all-reduce.2.cloned.1.call-done = f32[4,768,8]{1,2,0:T(8,128)} async-done(((f32[4,768,8]{1,2,0:T(8,128)}), f32[4,768,8]{1,2,0:T(8,128)}) %all-reduce.2.cloned.1.call-update) | async-done | bytes 98320 | tf_op jit(solution)/shard_map/psum | solution.py:43
  189.0 1.0 multiply_reduce_fusion
  190.0 1.1 fusion.9
  191.1 0.2 fusion.12
  191.2 0.0 copy-start.1
  191.3 4.4 %multiply_subtract_fusion = (f32[4,384,192]{1,2,0:T(8,128)}, f32[4,384,192]{1,2,0:T(8,128)}) fusion(f32[4,384,192]{1,2,0:T(8,128)} %param.6, f32[4,384,8]{1,2,0:T(8,128)S(1)} %add.45, f32[4,8,192]{2,1,0:T(8,128)S(1)} %fusion.12, f32[4,384,192]{1,2,0:T(8,128)} %param.7), kind=kOutput, calls=%fused_computation.7 | convolution fusion | flops 29786112 | bytes 4792320 | tf_op jit(solution)/shard_map/lir,lrw->liw/dot_general | solution.py:54
  195.6 0.0 copy-done.1
  195.6 0.7 broadcast_multiply_fusion
  (9 shorter events, 0.1 us)
Async XLA Ops:
  7.2 1.7 copy-start
  7.2 181.8 %all-reduce.2.cloned.1.call-start = ((), (), s32[]{:S(2)}) async-start(), calls=%async_computation | async-start | bytes 196608 | tf_op jit(solution)/shard_map/psum | solution.py:43
  10.4 4.1 %collective-permute-start = (f32[4,384,8]{1,2,0:T(8,128)S(1)}, f32[4,384,8]{1,2,0:T(8,128)S(1)}, u32[]{:S(2)}, u32[]{:S(2)}) collective-permute-start(f32[4,384,8]{1,2,0:T(8,128)S(1)} %fusion.2), channel_id=1, source_target_pairs={{0,8},{8,0},{16,24},{24,16},{1,9},{9,1},{17,25},{25,17},{2,10},{10... | collective-permute-start | bytes 147464 | tf_op jit(solution)/shard_map/ppermute | solution.py:17
  14.5 4.2 %collective-permute-start.1 = (f32[4,384,8]{1,2,0:T(8,128)S(1)}, f32[4,384,8]{1,2,0:T(8,128)S(1)}, u32[]{:S(2)}, u32[]{:S(2)}) collective-permute-start(f32[4,384,8]{1,2,0:T(8,128)S(1)} %add.44), channel_id=1, source_target_pairs={{0,16},{8,24},{16,0},{24,8},{1,17},{9,25},{17,1},{25,9},{2,18},{10... | collective-permute-start | bytes 147464 | tf_op jit(solution)/shard_map/ppermute | solution.py:17
  191.2 4.4 %copy-start.1 = (f32[4,768,8]{1,2,0:T(8,128)S(1)}, f32[4,768,8]{1,2,0:T(8,128)}, u32[]{:S(2)}) copy-start(f32[4,768,8]{1,2,0:T(8,128)} %all-reduce.2.cloned.1.call-done) | copy-start | bytes 294916
Sparse Core Ops, SparseCore 0:
  64.6 124.3 all-reduce.1
